TPU v7x, 32 devices: a whole 2x2x4 slice. The times are simulated.
32 devices in a mesh: img: 4 (over x, core), head: 2 (over y), txt: 4 (over z).
Axes of the slice: x: 2, y: 2, z: 4, core: 2. Of those that a mesh axis runs over, the one named last changes fastest.
Arguments:
- image_feats: bfloat16 [4096, 7680], P(('img', 'txt'), 'head'), may hold values from -6 to 6
- key_weight: bfloat16 [7680, 512], P('head'), may hold values from -0.0625 to 0.0625
- value_weight: bfloat16 [7680, 512], P('head'), may hold values from -0.0625 to 0.0625
- queries: bfloat16 [1024, 4096], P('txt', 'head'), may hold values from -21 to 21
- grad_out: bfloat16 [1024, 4096], P('txt', 'head'), may hold values from -768 to 768
- tile_image: int32 [32], P('img'), may hold values from 0 to 7, never falling along the last dimension, each value on 1 to 8 neighbouring positions
- text_sees: int32 [8, 8], replicated, may hold values from 0 to 1, as said below
Outputs:
- attn_out: bfloat16 [1024, 4096], P('txt', 'head')
- grad_feats: bfloat16 [4096, 7680], P(('img', 'txt'), 'head')
Inputs may be any that keep to these rules, and one draw needn't show every extreme that they name: `text_sees`: every row holds at least one 1.
All inputs are finite; a program needn't handle non-finite values.
Results may differ from a plain program's by a relative error of at most 0.012.
The roundings to bfloat16 on the way count: a program that leaves them out, or rounds other values in their place, can miss the bound.
Values may be sent and summed in bfloat16 or wider, within the bound.
A program may use at most 128 MiB of HBM per device.

v0:
```python
import functools
import math

import jax
import jax.numpy as jnp
from jax import lax
from jax.experimental import pallas as pl
from jax.experimental.pallas import tpu as pltpu
from jax.sharding import PartitionSpec as P

HD = 128
TILE = 128
TBLK = 128
MESH = pl.DeviceIdType.MESH
UNROLL = 4
LOG2E = 1.4426950408889634
NT = (((1,), (1,)), ((), ()))
F32 = jnp.float32
BF16 = jnp.bfloat16


def build_mask(text_sees, tile_image, text_count):
    blocks_total, images_total = text_sees.shape
    text_rows = lax.axis_index("txt") * text_count + jnp.arange(text_count, dtype=jnp.int32)
    block_onehot = (
        (text_rows // TBLK)[:, None] == jnp.arange(blocks_total, dtype=jnp.int32)[None, :]
    ).astype(F32)
    tile_onehot = (
        tile_image[:, None] == jnp.arange(images_total, dtype=jnp.int32)[None, :]
    ).astype(F32)
    tile_sees = jnp.dot(tile_onehot, text_sees.astype(F32).T)
    return jnp.dot(tile_sees, block_onehot.T)


def partner(me, step, count):
    if count & (count - 1):
        return lax.rem(me + step, count)
    other, bit = me, 1
    while bit < count:
        if step & bit:
            other = other + bit - 2 * bit * (lax.rem(other // bit, 2))
        bit *= 2
    return other


def receive_from(me, step, count):
    if count & (count - 1):
        return lax.rem(me - step + count, count)
    return partner(me, step, count)


def kernel(
    sizes,
    feats, kw, vw, q, g, mask,
    attn, dfeats,
    psend, precv, pacc, kvbuf, vtb, sbuf, numt, mst, tst, stbuf, lse, dlt, cown,
    osend, orecv, aout, gsend, grecv, gown, gacc, hall, grelay, facc,
    p_ss, p_rs, kv_ss, kv_rs, st_ss, st_rs, o_ss, o_rs, a_ss, a_rs, g_ss, g_rs, h_ss, h_rs,
    r_ss, gr_ss, gr_rs,
):
    ni, nh, nt = sizes
    img, hd, txt = lax.axis_index("img"), lax.axis_index("head"), lax.axis_index("txt")
    rows = feats.shape[0]
    groups = kvbuf.shape[1] // 2
    own_cols = groups * HD
    heads = q.shape[1] // HD
    reps = heads // groups
    block_tiles = rows // TILE
    share = osend.shape[1]
    relay = nt == 4
    inner = jnp.logical_or(txt == 1, txt == 2)
    outer = jnp.logical_not(inner)
    scale = 1.0 / math.sqrt(HD)
    unroll = math.gcd(UNROLL, reps)

    barrier = pltpu.get_barrier_semaphore()
    for step in range(1, nh):
        pl.semaphore_signal(barrier, inc=1, device_id={"head": lax.rem(hd + step, nh)}, device_id_type=MESH)
    for step in range(1, nt):
        pl.semaphore_signal(barrier, inc=1, device_id={"txt": lax.rem(txt + step, nt)}, device_id_type=MESH)
    for step in range(1, ni):
        pl.semaphore_signal(barrier, inc=1, device_id={"img": lax.rem(img + step, ni)}, device_id_type=MESH)
    pl.semaphore_wait(barrier, nh - 1 + nt - 1 + ni - 1)

    def remote(src, dst, ss, rs, axis, index):
        return pltpu.make_async_remote_copy(
            src_ref=src, dst_ref=dst, send_sem=ss, recv_sem=rs,
            device_id={axis: index}, device_id_type=MESH,
        )

    p_copies = []
    for step in range(1, nh):
        dest = lax.rem(hd + step, nh)
        cols = pl.ds(pl.multiple_of(dest * own_cols, own_cols), own_cols)
        for part, weight in enumerate((kw, vw)):
            psend[step - 1, part] = jnp.dot(
                feats[...], weight[:, cols], preferred_element_type=F32
            ).astype(BF16)
            copy = remote(
                psend.at[step - 1, part], precv.at[step - 1, part],
                p_ss.at[step - 1, part], p_rs.at[step - 1, part], "head", dest,
            )
            copy.start()
            p_copies.append(copy)
    cols = pl.ds(pl.multiple_of(hd * own_cols, own_cols), own_cols)
    for part, weight in enumerate((kw, vw)):
        pacc[part] = jnp.dot(feats[...], weight[:, cols], preferred_element_type=F32)
    kv_copies, relayed = [], []
    for part in range(2):
        total = pacc[part]
        for step in range(1, nh):
            p_copies[(step - 1) * 2 + part].wait_recv()
            total = total + precv[step - 1, part].astype(F32)
        total = total.astype(BF16)
        for group in range(groups):
            kvbuf[txt, part * groups + group] = total[:, group * HD : (group + 1) * HD]
        mine = kvbuf.at[txt, pl.ds(part * groups, groups)]
        for step in range(1, nt):
            copy = remote(
                mine, mine, kv_ss.at[step - 1, part], kv_rs.at[step - 1, part],
                "txt", partner(txt, step, nt),
            )
            if relay and step == 3:
                pl.when(inner)(copy.start)
            else:
                copy.start()
            kv_copies.append(copy)

    for step in range(nt):
        block = receive_from(txt, step, nt)
        if step:
            for part in range(2):
                kv_copies[part * (nt - 1) + step - 1].wait_recv()
                if relay and step == 2:
                    passed = kvbuf.at[block, pl.ds(part * groups, groups)]
                    copy = remote(
                        passed, passed, r_ss.at[part], kv_rs.at[2, part], "txt", partner(txt, 1, nt)
                    )
                    pl.when(inner)(copy.start)
                    relayed.append(copy)
        for group in range(groups):
            vtb[group] = kvbuf[block, groups + group].astype(F32).T.astype(BF16)

        def forward(turn, _, step=step, block=block):
            picked = [turn * unroll + i for i in range(unroll)]
            spans = [pl.ds(pl.multiple_of(head * HD, HD), HD) for head in picked]
            at = [pl.ds(head, 1) for head in picked]
            group = turn * unroll // reps
            keys, values_t = kvbuf[block, group], vtb[group]
            allowed = [
                mask[pl.ds(block * block_tiles + tile, 1), :] > 0.5 for tile in range(block_tiles)
            ]
            if step:
                before = [mst[row, :] for row in at]
                sums = [tst[row, :] for row in at]
                numers = [numt[head] for head in picked]
            kept, tops, totals, outs = [], [], [], []
            for i in range(unroll):
                scores = lax.dot_general(keys, q[:, spans[i]], NT, preferred_element_type=F32)
                scores = scores * (scale * LOG2E)
                masked = jnp.concatenate(
                    [
                        jnp.where(allowed[tile], scores[tile * TILE : (tile + 1) * TILE], -1e30)
                        for tile in range(block_tiles)
                    ],
                    axis=0,
                )
                top = jnp.max(masked, axis=0, keepdims=True)
                if step:
                    top = jnp.maximum(top, before[i])
                kept.append(masked)
                tops.append(top)
            for i in range(unroll):
                weights = jnp.exp2(kept[i] - tops[i]).astype(BF16)
                total = jnp.sum(weights.astype(F32), axis=0, keepdims=True)
                numer = jnp.dot(values_t, weights, preferred_element_type=F32)
                if step:
                    shrink = jnp.exp2(before[i] - tops[i])
                    total = total + sums[i] * shrink
                    numer = numer + numers[i] * shrink
                totals.append(total)
                outs.append(numer)
            for i in range(unroll):
                sbuf[step * heads + picked[i]] = kept[i]
                mst[at[i], :] = tops[i]
                tst[at[i], :] = totals[i]
                numt[picked[i]] = outs[i]
            return 0

        lax.fori_loop(0, heads // unroll, forward, 0)

    def deltas(head, _):
        cols = pl.ds(pl.multiple_of(head * HD, HD), HD)
        grad_t = g[:, cols].astype(F32).T
        row = pl.ds(head, 1)
        stbuf[img, 0, row, :] = mst[row, :]
        stbuf[img, 1, row, :] = tst[row, :]
        stbuf[img, 2, row, :] = jnp.sum(grad_t * numt[head], axis=0, keepdims=True)
        return 0

    lax.fori_loop(0, heads, deltas, 0)
    st_copies = []
    for step in range(1, ni):
        copy = remote(
            stbuf.at[img], stbuf.at[img], st_ss.at[step - 1], st_rs.at[step - 1],
            "img", lax.rem(img + step, ni),
        )
        copy.start()
        st_copies.append(copy)
    for copy in st_copies:
        copy.wait_recv()
    top = stbuf[0, 0]
    for i in range(1, ni):
        top = jnp.maximum(top, stbuf[i, 0])
    total = jnp.zeros_like(top)
    delta = jnp.zeros_like(top)
    for i in range(ni):
        factor = jnp.exp2(stbuf[i, 0] - top)
        total = total + factor * stbuf[i, 1]
        delta = delta + factor * stbuf[i, 2]
    lse[...] = top + jnp.log(total) * LOG2E
    dlt[...] = delta / total
    cown[...] = jnp.exp2(stbuf[img, 0] - top) / total

    def outputs(head, _):
        cols = pl.ds(pl.multiple_of(head * HD, HD), HD)
        piece = (numt[head] * cown[pl.ds(head, 1), :]).T.astype(BF16)
        for i in range(ni):
            osend[i, :, cols] = piece[i * share : (i + 1) * share]
        return 0

    lax.fori_loop(0, heads, outputs, 0)
    o_copies = []
    for step in range(1, ni):
        dest = lax.rem(img + step, ni)
        copy = remote(
            osend.at[dest], orecv.at[step - 1], o_ss.at[step - 1], o_rs.at[step - 1], "img", dest
        )
        copy.start()
        o_copies.append(copy)

    g_copies = []
    for step in range(nt - 1, -1, -1):
        block = receive_from(txt, step, nt)

        for group in range(groups):

            def backward(turn, _, step=step, block=block, group=group):
                picked = [group * reps + turn * unroll + i for i in range(unroll)]
                spans = [pl.ds(pl.multiple_of(head * HD, HD), HD) for head in picked]
                at = [pl.ds(head, 1) for head in picked]
                values = kvbuf[block, groups + group]
                key_grad, value_grad = gacc[0], gacc[1]
                grad_probs = [
                    lax.dot_general(values, g[:, cols], NT, preferred_element_type=F32)
                    for cols in spans
                ]
                for i in range(unroll):
                    probs = jnp.exp2(sbuf[step * heads + picked[i]] - lse[at[i], :])
                    grad_scores = (probs * (grad_probs[i] - dlt[at[i], :])).astype(BF16)
                    key_grad = key_grad + jnp.dot(
                        grad_scores, q[:, spans[i]], preferred_element_type=F32
                    )
                    value_grad = value_grad + jnp.dot(
                        probs.astype(BF16), g[:, spans[i]], preferred_element_type=F32
                    )
                gacc[0] = key_grad
                gacc[1] = value_grad
                return 0

            gacc[...] = jnp.zeros_like(gacc)
            lax.fori_loop(0, reps // unroll, backward, 0)
            if relay and step == 2:
                gown[group] = gacc[0] * scale
                gown[groups + group] = gacc[1]
            elif step:
                gsend[step - 1, group] = (gacc[0] * scale).astype(BF16)
                gsend[step - 1, groups + group] = gacc[1].astype(BF16)
            else:
                gown[group] = gacc[0] * scale
                gown[groups + group] = gacc[1]
        if relay and step == 2:

            def joined():
                relay_up.wait_recv()
                for part in range(2 * groups):
                    gsend[1, part] = (gown[part] + grelay[part].astype(F32)).astype(BF16)

            def alone():
                for part in range(2 * groups):
                    gsend[1, part] = gown[part].astype(BF16)

            pl.when(inner)(joined)
            pl.when(outer)(alone)
        if step:
            copy = remote(
                gsend.at[step - 1], grecv.at[step - 1], g_ss.at[step - 1], g_rs.at[step - 1],
                "txt", block,
            )
            if relay and step == 3:
                relay_up = remote(
                    gsend.at[2], grelay, gr_ss.at[0], gr_rs.at[0], "txt", partner(txt, 1, nt)
                )
                pl.when(inner)(copy.start)
                pl.when(outer)(relay_up.start)
                far = copy
            else:
                copy.start()
                g_copies.append(copy)

    for copy in o_copies:
        copy.wait_recv()
    rows_sum = osend[img].astype(F32)
    for step in range(1, ni):
        rows_sum = rows_sum + orecv[step - 1].astype(F32)
    aout[img] = rows_sum.astype(BF16)
    a_copies = []
    for step in range(1, ni):
        copy = remote(
            aout.at[img], aout.at[img], a_ss.at[step - 1], a_rs.at[step - 1],
            "img", lax.rem(img + step, ni),
        )
        copy.start()
        a_copies.append(copy)

    for copy in g_copies:
        copy.wait_recv()
    for part in range(2 * groups):
        total = gown[part]
        for step in range(1, 3 if relay else nt):
            total = total + grecv[step - 1, part].astype(F32)
        gown[part] = total
    if relay:

        def add_far():
            far.wait_recv()
            for part in range(2 * groups):
                gown[part] = gown[part] + grecv[2, part].astype(F32)

        pl.when(inner)(add_far)
    for part in range(2 * groups):
        hall[hd, part] = gown[part].astype(BF16)
    h_copies = []
    for step in range(1, nh):
        copy = remote(
            hall.at[hd], hall.at[hd], h_ss.at[step - 1], h_rs.at[step - 1],
            "head", lax.rem(hd + step, nh),
        )
        copy.start()
        h_copies.append(copy)
    width = feats.shape[1]
    chunk = math.gcd(width, 768)

    def features(owner):
        cols = pl.ds(pl.multiple_of(owner * own_cols, own_cols), own_cols)
        key_part = jnp.concatenate([hall[owner, i] for i in range(groups)], axis=1)
        value_part = jnp.concatenate([hall[owner, groups + i] for i in range(groups)], axis=1)

        def part(at):
            span = pl.ds(pl.multiple_of(at * chunk, chunk), chunk)
            return span, lax.dot_general(
                key_part, kw[span, cols], NT, preferred_element_type=F32
            ) + lax.dot_general(value_part, vw[span, cols], NT, preferred_element_type=F32)

        return part

    own_part = features(hd)

    def own_features(at, _):
        span, value = own_part(at)
        facc[:, span] = value
        return 0

    lax.fori_loop(0, width // chunk, own_features, 0)
    for step in range(1, nh):
        h_copies[step - 1].wait_recv()
        other_part = features(lax.rem(hd - step + nh, nh))

        def other_features(at, _, step=step, other_part=other_part):
            span, value = other_part(at)
            value = facc[:, span] + value
            if step == nh - 1:
                dfeats[:, span] = value.astype(BF16)
            else:
                facc[:, span] = value
            return 0

        lax.fori_loop(0, width // chunk, other_features, 0)

    for copy in a_copies:
        copy.wait_recv()
    for i in range(ni):
        attn[i] = aout[i]
    near = [copy for at, copy in enumerate(kv_copies) if not (relay and at % (nt - 1) == 2)]
    for copy in p_copies + near + st_copies + o_copies + g_copies + a_copies + h_copies:
        copy.wait_send()
    if relay:

        def inner_sends():
            for copy in [kv_copies[2], kv_copies[5], far] + relayed:
                copy.wait_send()

        pl.when(inner)(inner_sends)
        pl.when(outer)(relay_up.wait_send)


def shards(sizes, image_feats, key_weight, value_weight, queries, grad_out, tile_image, text_sees):
    ni, nh, nt = sizes
    rows = image_feats.shape[0]
    text, width = queries.shape
    heads = width // HD
    own_cols = key_weight.shape[1] // nh
    groups = own_cols // HD
    share = text // ni
    mask = build_mask(text_sees, tile_image, text)
    dma = pltpu.SemaphoreType.DMA
    vmem = pl.BlockSpec(memory_space=pltpu.VMEM)
    attn, grad_feats = pl.pallas_call(
        functools.partial(kernel, sizes),
        out_shape=(
            jax.ShapeDtypeStruct((ni, share, width), BF16),
            jax.ShapeDtypeStruct(image_feats.shape, BF16),
        ),
        in_specs=[vmem] * 6,
        out_specs=(vmem, vmem),
        scratch_shapes=[
            pltpu.VMEM((nh - 1, 2, rows, own_cols), BF16),
            pltpu.VMEM((nh - 1, 2, rows, own_cols), BF16),
            pltpu.VMEM((2, rows, own_cols), F32),
            pltpu.VMEM((nt, 2 * groups, rows, HD), BF16),
            pltpu.VMEM((groups, HD, rows), BF16),
            pltpu.VMEM((nt * heads, rows, text), F32),
            pltpu.VMEM((heads, HD, text), F32),
            pltpu.VMEM((heads, text), F32),
            pltpu.VMEM((heads, text), F32),
            pltpu.VMEM((ni, 3, heads, text), F32),
            pltpu.VMEM((heads, text), F32),
            pltpu.VMEM((heads, text), F32),
            pltpu.VMEM((heads, text), F32),
            pltpu.VMEM((ni, share, width), BF16),
            pltpu.VMEM((ni - 1, share, width), BF16),
            pltpu.VMEM((ni, share, width), BF16),
            pltpu.VMEM((nt - 1, 2 * groups, rows, HD), BF16),
            pltpu.VMEM((nt - 1, 2 * groups, rows, HD), BF16),
            pltpu.VMEM((2 * groups, rows, HD), F32),
            pltpu.VMEM((2, rows, HD), F32),
            pltpu.VMEM((nh, 2 * groups, rows, HD), BF16),
            pltpu.VMEM((2 * groups, rows, HD), BF16),
            pltpu.VMEM((rows, image_feats.shape[1]), F32),
            dma((nh - 1, 2)), dma((nh - 1, 2)),
            dma((nt - 1, 2)), dma((nt - 1, 2)),
            dma((ni - 1,)), dma((ni - 1,)),
            dma((ni - 1,)), dma((ni - 1,)),
            dma((ni - 1,)), dma((ni - 1,)),
            dma((nt - 1,)), dma((nt - 1,)),
            dma((nh - 1,)), dma((nh - 1,)),
            dma((2,)), dma((1,)), dma((1,)),
        ],
        compiler_params=pltpu.CompilerParams(
            collective_id=0, has_side_effects=True, vmem_limit_bytes=60 * 1024 * 1024
        ),
    )(image_feats, key_weight, value_weight, queries, grad_out, mask)
    return (attn.reshape(text, width), grad_feats)


def solution(mesh):
    sizes = (mesh.shape["img"], mesh.shape["head"], mesh.shape["txt"])
    placed = (
        P(("img", "txt"), "head"),
        P("head", None),
        P("head", None),
        P("txt", "head"),
        P("txt", "head"),
        P("img"),
        P(),
    )
    return jax.shard_map(
        functools.partial(shards, sizes),
        mesh=mesh,
        in_specs=placed,
        out_specs=(P("txt", "head"), P(("img", "txt"), "head")),
        check_vma=False,
    )
```

profile of v0, /device:TPU:0, one launch (start us, length us, event | category | flops | bytes accessed | tf_op | source)
XLA Modules:
  0.0 86.3 jit_solution(3370224738501536936)
XLA Ops:
  0.6 1.6 %fusion.mask = f32[8,256]{1,0:T(8,128)} fusion(s32[256]{0:T(256)S(1)} %and_select_fusion, s32[8,8]{1,0:T(8,128)} %param.13, s32[8]{0:T(128)} %param.12), kind=kOutput, calls=%fused_computation | convolution fusion | flops 35968 | bytes 9504 | tf_op jit(solution)/shard_map/dot_general | solution.py:32
  2.2 80.3 %shard_map.86 = (bf16[4,64,2048]{2,1,0:T(8,128)(2,1)}, bf16[256,3840]{1,0:T(8,128)(2,1)}) custom-call(bf16[256,3840]{1,0:T(8,128)(2,1)} %feats.1, bf16[3840,512]{1,0:T(8,128)(2,1)} %kw.1, bf16[3840,512]{1,0:T(8,128)(2,1)} %vw.1, bf16[256,2048]{1,0:T(8,128)(2,1)} %q.1, bf16[256,2048]{1,0:T(8,128)(2,1)} %g.1, f32[8,256]{1,0:T(8,128)} %fusion.mask), custom_call_target="tpu_custom_call" | custom-call | tf_op jit(solution)/shard_map/pallas_call | solution.py:418
  82.6 0.0 copy-start
  82.6 2.4 %copy.11 = bf16[256,2048]{1,0:T(8,128)(2,1)} copy(bf16[256,2048]{1,0:T(8,128)(2,1)} %bitcast.1) | data formatting | bytes 2097152
  85.0 0.0 copy-done
  85.0 1.3 %copy.12 = bf16[256,3840]{1,0:T(8,128)(2,1)} copy(bf16[256,3840]{1,0:T(8,128)(2,1)S(1)} %copy-done) | data formatting | bytes 3932160
  (1 shorter events, 0.0 us)
Async XLA Ops:
  82.6 2.5 %copy-start = (bf16[256,3840]{1,0:T(8,128)(2,1)S(1)}, bf16[256,3840]{1,0:T(8,128)(2,1)}, u32[]{:S(2)}) copy-start(bf16[256,3840]{1,0:T(8,128)(2,1)} %get-tuple-element.9) | copy-start | bytes 5898244
where the time goes:
time: 86.5 us; the launch traced here: 86.3 us
  Pallas kernels  80.3 us (93%)
  local copies, waits for them, and re-layouts  3.72 us (4%)
  matrix products  1.6 us (2%)
    pallas_call x1, Pallas kernels, shards(): pl.pallas_call(functools.partial(kernel, sizes), out_shape=(jax.ShapeDtyp...  80.3 us
    unnamed x4, local copies, waits for them, and re-layouts  3.72 us

commit v1 on v0

v1 whole, which is shorter than its diff:
```python
import functools
import math

import jax
import jax.numpy as jnp
from jax import lax
from jax.experimental import pallas as pl
from jax.experimental.pallas import tpu as pltpu
from jax.sharding import PartitionSpec as P

HD = 128
TILE = 128
TBLK = 128
MESH = pl.DeviceIdType.MESH
UNROLL = 4
LOG2E = 1.4426950408889634
NT = (((1,), (1,)), ((), ()))
F32 = jnp.float32
BF16 = jnp.bfloat16
HIDE = 2e30
FLOOR = -1e30
ONES = 16
VMEM_BUDGET = 58 * 1024 * 1024


def pick(index, table):
    value = jnp.int32(table[0])
    for at in range(1, len(table)):
        value = jnp.where(index == at, jnp.int32(table[at]), value)
    return value


def arrival_order(count):
    return [
        sorted((b for b in range(count) if b != z), key=lambda b: (abs(b - z), b))
        for z in range(count)
    ]


def departure_order(count):
    orders = []
    for z in range(count):
        above, below = list(range(count - 1, z, -1)), list(range(z))
        orders.append((above + below if 2 * z < count else below + above[::-1]) + [z])
    return orders


def kernel(
    sizes, keep,
    feats_hbm, kw_hbm, vw_hbm, q_hbm, g_hbm, tile_image, text_sees,
    attn, dfeats,
    feats, kw, vw, qraw, graw, qt, gt, big, psend, precv, pacc, kvbuf, vtb, sbuf, numt, mst, tst,
    stbuf, lse, dlt, cown, gsend, grecv, gpart, hall, ocr, xs, xr,
    l_s, w_s, p_ss, p_rs, kv_ss, kv_fs, kv_rs, st_ss, st_rs, oc_ss, oc_rs, ox_ss, ox_rs,
    oa_ss, oa_rs, g_ss, g_rs, h_ss, h_rs,
):
    ni, nh, nt = sizes
    img, hd, txt = lax.axis_index("img"), lax.axis_index("head"), lax.axis_index("txt")
    rows, width = feats.shape
    groups = kvbuf.shape[0]
    own_cols = groups * HD
    text = qraw.shape[0]
    heads = qraw.shape[1] // HD
    reps = heads // groups
    block_tiles = rows // TILE
    scale = 1.0 / math.sqrt(HD)
    unroll = math.gcd(UNROLL, reps)
    half = text // 2
    gcols = reps * HD
    bits = ni.bit_length() - 1
    arrive, depart = arrival_order(nt), departure_order(nt)

    def cols_of(owner, group):
        return pl.ds(pl.multiple_of(owner * own_cols + group * HD, HD), HD)

    def other(step):
        return lax.rem(hd + step, nh)

    loads = [pltpu.make_async_copy(feats_hbm, feats, l_s.at[0])]
    weight_loads = {}
    for step in list(range(1, nh)) + [0]:
        for group in range(groups):
            cols = cols_of(other(step), group)
            pair = [
                pltpu.make_async_copy(src.at[:, cols], dst.at[:, cols], w_s.at[step, group, part])
                for part, (src, dst) in enumerate(((kw_hbm, kw), (vw_hbm, vw)))
            ]
            weight_loads[step, group] = pair
            loads += pair
    q_load = pltpu.make_async_copy(q_hbm, qraw, l_s.at[1])
    g_load = pltpu.make_async_copy(g_hbm, graw, l_s.at[2])
    loads += [q_load, g_load]
    for copy in loads:
        copy.start()

    barrier = pltpu.get_barrier_semaphore()
    for step in range(1, nh):
        pl.semaphore_signal(barrier, inc=1, device_id={"head": other(step)}, device_id_type=MESH)
    for step in range(1, nt):
        pl.semaphore_signal(barrier, inc=1, device_id={"txt": lax.rem(txt + step, nt)}, device_id_type=MESH)
    for step in range(1, ni):
        pl.semaphore_signal(barrier, inc=1, device_id={"img": lax.rem(img + step, ni)}, device_id_type=MESH)

    def remote(src, dst, ss, rs, axis, index):
        return pltpu.make_async_remote_copy(
            src_ref=src, dst_ref=dst, send_sem=ss, recv_sem=rs,
            device_id={axis: index}, device_id_type=MESH,
        )

    first_block = txt * (text // TBLK)
    for tile in range(big.shape[0]):
        image = tile_image[tile]
        parts = [
            jnp.full((1, TBLK), text_sees[first_block + at, image].astype(F32))
            for at in range(text // TBLK)
        ]
        seen = jnp.concatenate(parts, axis=1)
        big[pl.ds(tile, 1), :] = jnp.where(seen > 0.5, 0.0, HIDE)
    vtb[pl.ds(HD, ONES), :] = jnp.ones((ONES, rows), BF16)

    def project(step, group):
        for copy in weight_loads[step, group]:
            copy.wait()
        cols = cols_of(other(step), group)
        weights = jnp.concatenate([kw[:, cols], vw[:, cols]], axis=1)
        return jnp.dot(feats[...], weights, preferred_element_type=F32)

    loads[0].wait()
    p_copies = {}
    for step in range(1, nh):
        for group in range(groups):
            value = project(step, group).astype(BF16)
            if step == 1 and group == 0:
                pl.semaphore_wait(barrier, nh - 1 + nt - 1 + ni - 1)
            for part in range(2):
                psend[step - 1, group, part] = value[:, part * HD : (part + 1) * HD]
                at = (step - 1, group, part)
                copy = remote(
                    psend.at[at], precv.at[at], p_ss.at[at], p_rs.at[at], "head", other(step)
                )
                copy.start()
                p_copies[at] = copy
    for group in range(groups):
        pacc[group] = project(0, group)

    def kv_copy(group, part, side):
        mine = kvbuf.at[group, txt, part]
        return remote(
            mine, mine, kv_ss.at[group, part, side], kv_rs.at[group, txt, part],
            "txt", txt + (1, -1)[side],
        )

    has_side = (txt < nt - 1, txt > 0)

    def own_sum(group, part):
        total = pacc[group, :, part * HD : (part + 1) * HD]
        for step in range(1, nh):
            p_copies[step - 1, group, part].wait_recv()
            total = total + precv[step - 1, group, part].astype(F32)
        kvbuf[group, txt, part] = total.astype(BF16)

    last_pass = [
        [max([0] + [s + 1 for s, b in enumerate(arrive[z]) if (b < z) == (side == 0)]) for z in range(nt)]
        for side in range(2)
    ]

    def send_own(group, after):
        for side in range(2):
            now = has_side[side]
            if after is not None:
                now = jnp.logical_and(now, pick(txt, last_pass[side]) == after)

            def go(side=side):
                for part in range(2):
                    kv_copy(group, part, side).start()

            pl.when(now)(go)

    def arrival(group, step):
        block = pick(txt, [arrive[z][step - 1] for z in range(nt)])
        onward = jnp.where(block < txt, txt + 1, txt - 1)
        valid = jnp.logical_and(onward >= 0, onward < nt)
        copies = []
        for part in range(2):
            there = kvbuf.at[group, block, part]
            copies.append(
                remote(
                    there, there, kv_fs.at[group, step, part], kv_rs.at[group, block, part],
                    "txt", onward,
                )
            )
        return block, valid, copies

    def receive(group, step):
        _, valid, copies = arrival(group, step)
        for copy in copies:
            copy.wait_recv()
            pl.when(valid)(copy.start)

    def turn_over(group):
        def body(at, _):
            head = group * reps + at
            cols = pl.ds(pl.multiple_of(head * HD, HD), HD)
            qt[head] = qraw[:, cols].astype(F32).T.astype(BF16)
            gt[head] = graw[:, cols].astype(F32).T.astype(BF16)
            return 0

        lax.fori_loop(0, reps, body, 0)

    def scaled_scores(keys, head):
        return jnp.dot(keys, qt[head], preferred_element_type=F32) * (scale * LOG2E)

    def tiles_of(array):
        return [array[t * TILE : (t + 1) * TILE] for t in range(block_tiles)]

    def slot(group, block, at):
        return (group * nt + block) * reps + at

    def forward(group, block, first):
        vtb[pl.ds(0, HD), :] = kvbuf[group, block, 1].astype(F32).T.astype(BF16)

        def body(turn, _):
            at = [turn * unroll + i for i in range(unroll)]
            keys, values_t = kvbuf[group, block, 0], vtb[...]
            hide = [big[pl.ds(block * block_tiles + t, 1), :] for t in range(block_tiles)]
            kept, tops, totals, outs = [], [], [], []
            for i in range(unroll):
                head = group * reps + at[i]
                scores = scaled_scores(keys, head)
                if keep:
                    sbuf[slot(group, block, at[i])] = scores
                top = jnp.full((1, text), FLOOR, F32) if first else mst[pl.ds(head, 1), :]
                for t, part in enumerate(tiles_of(scores)):
                    top = jnp.maximum(top, jnp.max(part, axis=0, keepdims=True) - hide[t])
                kept.append(scores)
                tops.append(top)
            for i in range(unroll):
                head = group * reps + at[i]
                weights = jnp.concatenate(
                    [jnp.exp2(part - (tops[i] + hide[t])) for t, part in enumerate(tiles_of(kept[i]))],
                    axis=0,
                ).astype(BF16)
                both = jnp.dot(values_t, weights, preferred_element_type=F32)
                numer, total = both[:HD], both[HD : HD + 1]
                if not first:
                    shrink = jnp.exp2(mst[pl.ds(head, 1), :] - tops[i])
                    total = total + tst[pl.ds(head, 1), :] * shrink
                    numer = numer + numt[head] * shrink
                totals.append(total)
                outs.append(numer)
            for i in range(unroll):
                head = group * reps + at[i]
                mst[pl.ds(head, 1), :] = tops[i]
                tst[pl.ds(head, 1), :] = totals[i]
                numt[head] = outs[i]
            return 0

        lax.fori_loop(0, reps // unroll, body, 0)

    def group_rows(group):
        return pl.ds(group * reps, reps)

    def stats_copies(group):
        return [
            remote(
                stbuf.at[group, img], stbuf.at[group, img], st_ss.at[group, step - 1],
                st_rs.at[group, step - 1], "img", lax.rem(img + step, ni),
            )
            for step in range(1, ni)
        ]

    def stats_start(group):
        def deltas(at, _):
            head = group * reps + at
            stbuf[group, img, 2, pl.ds(at, 1), :] = jnp.sum(
                gt[head].astype(F32) * numt[head], axis=0, keepdims=True
            )
            return 0

        lax.fori_loop(0, reps, deltas, 0)
        stbuf[group, img, 0] = mst[group_rows(group), :]
        stbuf[group, img, 1] = tst[group_rows(group), :]
        for copy in stats_copies(group):
            copy.start()

    def stats_finish(group):
        for copy in stats_copies(group):
            copy.wait_recv()
        top = stbuf[group, 0, 0]
        for i in range(1, ni):
            top = jnp.maximum(top, stbuf[group, i, 0])
        total = jnp.zeros_like(top)
        delta = jnp.zeros_like(top)
        for i in range(ni):
            factor = jnp.exp2(stbuf[group, i, 0] - top)
            total = total + factor * stbuf[group, i, 1]
            delta = delta + factor * stbuf[group, i, 2]
        lse[group_rows(group), :] = top + jnp.log(total) * LOG2E
        dlt[group_rows(group), :] = delta / total
        cown[group_rows(group), :] = jnp.exp2(stbuf[group, img, 0] - top) / total

    def goal(step):
        return pick(txt, [depart[z][step] for z in range(nt)])

    def grad_copy(group, step, part):
        block = goal(step)
        up = block > txt
        target = jnp.where(up, txt + 1, txt - 1)
        back = jnp.where(up, txt - 1, txt + 1)
        lands = jnp.where(jnp.logical_and(target == block, jnp.logical_not(up)), nt, block)
        copy = remote(
            gsend.at[group, step, part], grecv.at[group, lands, part],
            g_ss.at[group, step, part], g_rs.at[group, lands, part], "txt", target,
        )
        relayed = jnp.logical_and(back >= 0, back < nt)
        return copy, relayed, block

    def grad_wait(group, place, part):
        remote(
            gsend.at[group, 0, part], grecv.at[group, place, part],
            g_ss.at[group, 0, part], g_rs.at[group, place, part], "txt", txt,
        ).wait_recv()

    def backward(group, step):
        block = goal(step)

        def body(turn, _):
            at = [turn * unroll + i for i in range(unroll)]
            keys, values = kvbuf[group, block, 0], kvbuf[group, block, 1]
            hide = [big[pl.ds(block * block_tiles + t, 1), :] for t in range(block_tiles)]
            probs_all, grads_all = [], []
            for i in range(unroll):
                head = group * reps + at[i]
                grad_probs = jnp.dot(values, gt[head], preferred_element_type=F32)
                if keep:
                    scores = sbuf[slot(group, block, at[i])]
                else:
                    scores = scaled_scores(keys, head)
                base = lse[pl.ds(head, 1), :]
                probs = jnp.concatenate(
                    [jnp.exp2(part - (base + hide[t])) for t, part in enumerate(tiles_of(scores))],
                    axis=0,
                )
                grads_all.append((probs * (grad_probs - dlt[pl.ds(head, 1), :])).astype(BF16))
                probs_all.append(probs.astype(BF16))
            picked = [group * reps + a for a in at]
            queries = jnp.concatenate([qt[head] for head in picked], axis=1)
            grads = jnp.concatenate([gt[head] for head in picked], axis=1)
            gpart[step, 0] = gpart[step, 0] + lax.dot_general(
                queries, jnp.concatenate(grads_all, axis=1), NT, preferred_element_type=F32
            )
            gpart[step, 1] = gpart[step, 1] + lax.dot_general(
                grads, jnp.concatenate(probs_all, axis=1), NT, preferred_element_type=F32
            )
            return 0

        gpart[step] = jnp.zeros_like(gpart[step])
        lax.fori_loop(0, reps // unroll, body, 0)

    def grown(step, part):
        value = gpart[step, part]
        return value * scale if part == 0 else value

    def leave(group, step):
        for part in range(2):
            copy, relayed, _ = grad_copy(group, step, part)

            def go(copy=copy, part=part):
                gsend[group, step, part] = grown(step, part).astype(BF16)
                copy.start()

            pl.when(jnp.logical_not(relayed))(go)

    def pass_on(group, step):
        for part in range(2):
            copy, relayed, block = grad_copy(group, step, part)

            def go(copy=copy, part=part, block=block):
                grad_wait(group, block, part)
                gsend[group, step, part] = (
                    grown(step, part) + grecv[group, block, part].astype(F32)
                ).astype(BF16)
                copy.start()

            pl.when(relayed)(go)

    def h_copy(step, group, part):
        mine = hall.at[hd, group, part]
        at = (step - 1, group, part)
        return remote(mine, mine, h_ss.at[at], h_rs.at[at], "head", other(step))

    def own_grad(group):
        for part in range(2):
            gpart[nt - 1, part] = grown(nt - 1, part)
            for there, place in ((txt > 0, txt), (txt < nt - 1, jnp.int32(nt))):

                def add(place=place, part=part):
                    grad_wait(group, place, part)
                    gpart[nt - 1, part] = gpart[nt - 1, part] + grecv[group, place, part].astype(F32)

                pl.when(there)(add)
            hall[hd, group, part] = gpart[nt - 1, part].T.astype(BF16)
            for step in range(1, nh):
                h_copy(step, group, part).start()

    lower = lax.rem(img, 2)
    mate = img + 1 - 2 * lower
    mine_rows = pl.ds(pl.multiple_of(lower * half, half), half)
    mate_rows = pl.ds(pl.multiple_of((1 - lower) * half, half), half)

    def flip(bit):
        return img + (1 << bit) - (2 << bit) * lax.rem(img // (1 << bit), 2)

    def out_cols(group):
        return pl.ds(group * gcols, gcols)

    def pair_copy(group):
        return remote(
            qraw.at[mate_rows, out_cols(group)], ocr.at[group], oc_ss.at[group], oc_rs.at[group],
            "img", mate,
        )

    def cross_copy(group, bit):
        at = (group, bit - 1)
        return remote(xs.at[at], xr.at[at], ox_ss.at[at], ox_rs.at[at], "img", flip(bit))

    def share_copy(group):
        there = graw.at[mine_rows, out_cols(group)]
        return remote(there, there, oa_ss.at[group], oa_rs.at[group], "img", mate)

    def outputs(group):
        def body(at, _):
            head = group * reps + at
            cols = pl.ds(pl.multiple_of(head * HD, HD), HD)
            qraw[:, cols] = (numt[head] * cown[pl.ds(head, 1), :]).T.astype(BF16)
            return 0

        lax.fori_loop(0, reps, body, 0)
        pair_copy(group).start()

    def cross(group):
        pair_copy(group).wait_recv()
        total = qraw[mine_rows, out_cols(group)].astype(F32) + ocr[group].astype(F32)
        if bits > 1:
            xs[group, 0] = total.astype(BF16)
            cross_copy(group, 1).start()
        else:
            graw[mine_rows, out_cols(group)] = total.astype(BF16)
            share_copy(group).start()

    def share(group):
        for bit in range(1, bits):
            cross_copy(group, bit).wait_recv()
            total = (xs[group, bit - 1].astype(F32) + xr[group, bit - 1].astype(F32)).astype(BF16)
            if bit < bits - 1:
                xs[group, bit] = total
                cross_copy(group, bit + 1).start()
            else:
                graw[mine_rows, out_cols(group)] = total
                share_copy(group).start()

    def finish_output(group):
        share_copy(group).wait_recv()
        attn[:, out_cols(group)] = graw[:, out_cols(group)]

    per = math.gcd(width // text, 3)
    chunk = per * text

    def features(pairs, first, last):
        def body(at, _):
            span = pl.ds(pl.multiple_of(at * chunk, chunk), chunk)
            left = jnp.concatenate([hall[o, group, p] for o, group in pairs for p in range(2)], axis=1)
            right = jnp.concatenate(
                [w[span, cols_of(o, group)] for o, group in pairs for w in (kw, vw)], axis=1
            )
            value = lax.dot_general(left, right, NT, preferred_element_type=F32)
            for j in range(per):
                piece = value[:, j * text : (j + 1) * text]
                if not first:
                    piece = piece + sbuf[at * per + j]
                if last:
                    start = pl.multiple_of(at * chunk + j * text, text)
                    dfeats[:, pl.ds(start, text)] = piece.astype(BF16)
                else:
                    sbuf[at * per + j] = piece
            return 0

        lax.fori_loop(0, width // chunk, body, 0)

    def h_wait(group):
        for step in range(1, nh):
            for part in range(2):
                h_copy(step, group, part).wait_recv()

    for part in range(2):
        own_sum(0, part)

        def go(part=part, side=0):
            kv_copy(0, part, side).start()

        for side in range(2):
            pl.when(has_side[side])(functools.partial(go, part, side))
    q_load.wait()
    g_load.wait()
    turn_over(0)
    forward(0, txt, True)
    for part in range(2):
        own_sum(1, part)
    send_own(1, 0)
    for step in range(1, nt):
        receive(0, step)
        send_own(1, step)
        forward(0, arrival(0, step)[0], False)
        if step == 1:
            turn_over(1)
    stats_start(0)
    forward(1, txt, True)
    receive(1, 1)
    stats_finish(0)
    for step in range(nt - 1):
        backward(0, step)
        leave(0, step)
        if step + 2 < nt:
            receive(1, step + 2)
        if step >= 1:
            pass_on(0, step - 1)
    for step in range(1, nt):
        forward(1, arrival(1, step)[0], False)
    stats_start(1)
    pass_on(0, nt - 2)
    backward(0, nt - 1)
    outputs(0)
    stats_finish(1)
    for step in range(nt - 1):
        if step == 1:
            own_grad(0)
            outputs(1)
            cross(0)
        backward(1, step)
        leave(1, step)
        if step >= 1:
            pass_on(1, step - 1)
    backward(1, nt - 1)
    pass_on(1, nt - 2)
    cross(1)
    share(0)
    h_wait(0)
    owners = [hd] + [other(step) for step in range(1, nh)]
    features([(o, 0) for o in owners], True, False)
    own_grad(1)
    features([(hd, 1)], False, False)
    share(1)
    finish_output(0)
    finish_output(1)
    h_wait(1)
    features([(o, 1) for o in owners[1:]], False, True)

    for copy in p_copies.values():
        copy.wait_send()
    for group in range(groups):
        for side in range(2):

            def own_sent(group=group, side=side):
                for part in range(2):
                    kv_copy(group, part, side).wait_send()

            pl.when(has_side[side])(own_sent)
        for step in range(1, nt):
            _, valid, copies = arrival(group, step)

            def passed(copies=copies):
                for copy in copies:
                    copy.wait_send()

            pl.when(valid)(passed)
        for copy in stats_copies(group):
            copy.wait_send()
        for step in range(nt - 1):
            for part in range(2):
                grad_copy(group, step, part)[0].wait_send()
        pair_copy(group).wait_send()
        for bit in range(1, bits):
            cross_copy(group, bit).wait_send()
        share_copy(group).wait_send()
        for step in range(1, nh):
            for part in range(2):
                h_copy(step, group, part).wait_send()


def shards(sizes, image_feats, key_weight, value_weight, queries, grad_out, tile_image, text_sees):
    ni, nh, nt = sizes
    rows, feat_width = image_feats.shape
    text, width = queries.shape
    heads = width // HD
    own_cols = key_weight.shape[1] // nh
    groups = own_cols // HD
    reps = heads // groups
    half = text // 2
    gcols = reps * HD
    tiles = nt * rows // TILE
    crosses = max(ni.bit_length() - 2, 1)
    slots = feat_width // text
    keep = nt * heads * rows * text * 4 <= VMEM_BUDGET // 3
    if keep:
        slots = max(slots, nt * heads)
    dma = pltpu.SemaphoreType.DMA
    hbm = pl.BlockSpec(memory_space=pl.ANY)
    vmem = pl.BlockSpec(memory_space=pltpu.VMEM)
    smem = pl.BlockSpec(memory_space=pltpu.SMEM)
    attn, grad_feats = pl.pallas_call(
        functools.partial(kernel, sizes, keep),
        out_shape=(
            pltpu.VMEM((text, width), BF16),
            pltpu.VMEM(image_feats.shape, BF16),
        ),
        in_specs=[hbm] * 5 + [smem] * 2,
        out_specs=(vmem, vmem),
        scratch_shapes=[
            pltpu.VMEM(image_feats.shape, BF16),
            pltpu.VMEM(key_weight.shape, BF16),
            pltpu.VMEM(value_weight.shape, BF16),
            pltpu.VMEM((text, width), BF16),
            pltpu.VMEM((text, width), BF16),
            pltpu.VMEM((heads, HD, text), BF16),
            pltpu.VMEM((heads, HD, text), BF16),
            pltpu.VMEM((tiles, text), F32),
            pltpu.VMEM((nh - 1, groups, 2, rows, HD), BF16),
            pltpu.VMEM((nh - 1, groups, 2, rows, HD), BF16),
            pltpu.VMEM((groups, rows, 2 * HD), F32),
            pltpu.VMEM((groups, nt, 2, rows, HD), BF16),
            pltpu.VMEM((HD + ONES, rows), BF16),
            pltpu.VMEM((slots, rows, text), F32),
            pltpu.VMEM((heads, HD, text), F32),
            pltpu.VMEM((heads, text), F32),
            pltpu.VMEM((heads, text), F32),
            pltpu.VMEM((groups, ni, 3, reps, text), F32),
            pltpu.VMEM((heads, text), F32),
            pltpu.VMEM((heads, text), F32),
            pltpu.VMEM((heads, text), F32),
            pltpu.VMEM((groups, nt - 1, 2, HD, rows), BF16),
            pltpu.VMEM((groups, nt + 1, 2, HD, rows), BF16),
            pltpu.VMEM((nt, 2, HD, rows), F32),
            pltpu.VMEM((nh, groups, 2, rows, HD), BF16),
            pltpu.VMEM((groups, half, gcols), BF16),
            pltpu.VMEM((groups, crosses, half, gcols), BF16),
            pltpu.VMEM((groups, crosses, half, gcols), BF16),
            dma((3,)), dma((nh, groups, 2)),
            dma((nh - 1, groups, 2)), dma((nh - 1, groups, 2)),
            dma((groups, 2, 2)), dma((groups, nt, 2)), dma((groups, nt, 2)),
            dma((groups, ni - 1)), dma((groups, ni - 1)),
            dma((groups,)), dma((groups,)),
            dma((groups, crosses)), dma((groups, crosses)),
            dma((groups,)), dma((groups,)),
            dma((groups, nt - 1, 2)), dma((groups, nt + 1, 2)),
            dma((nh - 1, groups, 2)), dma((nh - 1, groups, 2)),
        ],
        compiler_params=pltpu.CompilerParams(
            collective_id=0, has_side_effects=True, vmem_limit_bytes=VMEM_BUDGET
        ),
    )(image_feats, key_weight, value_weight, queries, grad_out, tile_image, text_sees)
    return (attn, grad_feats)


def solution(mesh):
    sizes = (mesh.shape["img"], mesh.shape["head"], mesh.shape["txt"])
    placed = (
        P(("img", "txt"), "head"),
        P("head", None),
        P("head", None),
        P("txt", "head"),
        P("txt", "head"),
        P("img"),
        P(),
    )
    return jax.shard_map(
        functools.partial(shards, sizes),
        mesh=mesh,
        in_specs=placed,
        out_specs=(P("txt", "head"), P(("img", "txt"), "head")),
        check_vma=False,
    )
```

time: 86.5 us -> 69.3 us (0.80)
  Pallas kernels: 80.3 us -> 65.5 us
  matrix products: 1.6 us -> 0 us
  local copies, waits for them, and re-layouts: 3.72 us -> 2.24 us
    pallas_call x1, Pallas kernels: 80.3 us -> 65.5 us  [shards(): pl.pallas_call(functools.partial(kernel, sizes, keep), out_shape=(pltpu.V...]
    dot_general x1 -> x0, matrix products: 1.6 us -> none  [build_mask(): return jnp.dot(tile_sees, block_onehot.T)]
    unnamed x4 -> x2, local copies, waits for them, and re-layouts: 3.72 us -> 2.24 us
where the time goes in v1:
time: 69.3 us; the launch traced here: 68.4 us
  Pallas kernels  65.5 us (95%)
  local copies, waits for them, and re-layouts  2.24 us (3%)
    pallas_call x1, Pallas kernels, shards(): pl.pallas_call(functools.partial(kernel, sizes, keep), out_shape=(pltpu.V...  65.5 us
    unnamed x2, local copies, waits for them, and re-layouts  2.24 us

profile of v1, /device:TPU:0, one launch (start us, length us, event | category | flops | bytes accessed | tf_op | source)
XLA Modules:
  0.0 68.4 jit_solution(12676100833087822599)
XLA Ops:
  0.6 65.5 %shard_map.86 = (bf16[256,2048]{1,0:T(8,128)(2,1)S(1)}, bf16[256,3840]{1,0:T(8,128)(2,1)S(1)}) custom-call(bf16[256,3840]{1,0:T(8,128)(2,1)} %feats_hbm.1, bf16[3840,512]{1,0:T(8,128)(2,1)} %kw_hbm.1, bf16[3840,512]{1,0:T(8,128)(2,1)} %vw_hbm.1, bf16[256,2048]{1,0:T(8,128)(2,1)} %q_hbm.1, bf16[256,2048]{1,0:T(8,128)(2,1)} %g_hbm.1, s32[8]{0:T(128)} %tile_image.1, ...), custom_call_target="tpu_custom_call" | custom-call | tf_op jit(solution)/shard_map/pallas_call | solution.py:610
  66.2 1.0 %copy.11 = bf16[256,2048]{1,0:T(8,128)(2,1)} copy(bf16[256,2048]{1,0:T(8,128)(2,1)S(1)} %get-tuple-element.2) | data formatting | bytes 2097152
  67.1 1.3 %copy.12 = bf16[256,3840]{1,0:T(8,128)(2,1)} copy(bf16[256,3840]{1,0:T(8,128)(2,1)S(1)} %get-tuple-element.3) | data formatting | bytes 3932160

commit v2 on v1

--- a/solution.py
+++ b/solution.py
@@ -69,6 +69,9 @@
     gcols = reps * HD
     bits = ni.bit_length() - 1
     arrive, depart = arrival_order(nt), departure_order(nt)
+    relay = nt == 4
+    inner = jnp.logical_or(txt == 1, txt == 2)
+    outer = jnp.logical_not(inner)
 
     def cols_of(owner, group):
         return pl.ds(pl.multiple_of(owner * own_cols + group * HD, HD), HD)
@@ -143,15 +146,6 @@
     for group in range(groups):
         pacc[group] = project(0, group)
 
-    def kv_copy(group, part, side):
-        mine = kvbuf.at[group, txt, part]
-        return remote(
-            mine, mine, kv_ss.at[group, part, side], kv_rs.at[group, txt, part],
-            "txt", txt + (1, -1)[side],
-        )
-
-    has_side = (txt < nt - 1, txt > 0)
-
     def own_sum(group, part):
         total = pacc[group, :, part * HD : (part + 1) * HD]
         for step in range(1, nh):
@@ -159,43 +153,58 @@
             total = total + precv[step - 1, group, part].astype(F32)
         kvbuf[group, txt, part] = total.astype(BF16)
 
-    last_pass = [
-        [max([0] + [s + 1 for s, b in enumerate(arrive[z]) if (b < z) == (side == 0)]) for z in range(nt)]
-        for side in range(2)
-    ]
-
-    def send_own(group, after):
-        for side in range(2):
-            now = has_side[side]
-            if after is not None:
-                now = jnp.logical_and(now, pick(txt, last_pass[side]) == after)
-
-            def go(side=side):
-                for part in range(2):
-                    kv_copy(group, part, side).start()
-
-            pl.when(now)(go)
-
-    def arrival(group, step):
-        block = pick(txt, [arrive[z][step - 1] for z in range(nt)])
-        onward = jnp.where(block < txt, txt + 1, txt - 1)
-        valid = jnp.logical_and(onward >= 0, onward < nt)
-        copies = []
+    near = [[b for b in arrive[z] if not (relay and abs(b - z) == 3)] for z in range(nt)]
+    most = max(len(places) for places in near)
+
+    def own_copies(group, part):
+        mine = kvbuf.at[group, txt, part]
+        for at in range(most):
+            there = pick(txt, [places[at] if at < len(places) else -1 for places in near])
+            yield there >= 0, remote(
+                mine, mine, kv_ss.at[group, part, at], kv_rs.at[group, txt, part], "txt", there
+            )
+
+    def send_own(group, parts):
+        for part in parts:
+            for valid, copy in own_copies(group, part):
+                pl.when(valid)(copy.start)
+
+    def block_at(step):
+        return pick(txt, [arrive[z][step - 1] for z in range(nt)])
+
+    def relay_copy(group, part):
+        there = kvbuf.at[group, block_at(nt - 1), part]
+        return remote(
+            there, there, kv_fs.at[group, part], kv_rs.at[group, block_at(nt - 1), part],
+            "txt", jnp.where(txt == 1, 0, nt - 1),
+        )
+
+    def receive(group, step):
+        block = block_at(step)
         for part in range(2):
             there = kvbuf.at[group, block, part]
-            copies.append(
-                remote(
-                    there, there, kv_fs.at[group, step, part], kv_rs.at[group, block, part],
-                    "txt", onward,
-                )
-            )
-        return block, valid, copies
-
-    def receive(group, step):
-        _, valid, copies = arrival(group, step)
-        for copy in copies:
-            copy.wait_recv()
-            pl.when(valid)(copy.start)
+            remote(
+                there, there, kv_ss.at[group, part, 0], kv_rs.at[group, block, part], "txt", txt
+            ).wait_recv()
+
+    def pass_block(group, then=None):
+        def go():
+            for part in range(2):
+                relay_copy(group, part).wait_recv()
+                relay_copy(group, part).start()
+            if then is not None:
+                then()
+
+        if relay:
+            pl.when(inner)(go)
+        elif then is not None:
+            then()
+
+    def receive_last(group):
+        if relay:
+            pl.when(outer)(lambda: receive(group, nt - 1))
+        else:
+            receive(group, nt - 1)
 
     def turn_over(group):
         def body(at, _):
@@ -303,17 +312,14 @@
         return pick(txt, [depart[z][step] for z in range(nt)])
 
     def grad_copy(group, step, part):
-        block = goal(step)
-        up = block > txt
-        target = jnp.where(up, txt + 1, txt - 1)
-        back = jnp.where(up, txt - 1, txt + 1)
-        lands = jnp.where(jnp.logical_and(target == block, jnp.logical_not(up)), nt, block)
-        copy = remote(
+        target, lands = goal(step), txt
+        if relay and step == 0:
+            target = pick(txt, [1, nt - 1, 0, 2])
+            lands = jnp.where(outer, nt, txt)
+        return remote(
             gsend.at[group, step, part], grecv.at[group, lands, part],
             g_ss.at[group, step, part], g_rs.at[group, lands, part], "txt", target,
         )
-        relayed = jnp.logical_and(back >= 0, back < nt)
-        return copy, relayed, block
 
     def grad_wait(group, place, part):
         remote(
@@ -362,27 +368,27 @@
         return value * scale if part == 0 else value
 
     def leave(group, step):
-        for part in range(2):
-            copy, relayed, _ = grad_copy(group, step, part)
-
-            def go(copy=copy, part=part):
+        def go():
+            for part in range(2):
                 gsend[group, step, part] = grown(step, part).astype(BF16)
-                copy.start()
-
-            pl.when(jnp.logical_not(relayed))(go)
-
-    def pass_on(group, step):
-        for part in range(2):
-            copy, relayed, block = grad_copy(group, step, part)
-
-            def go(copy=copy, part=part, block=block):
-                grad_wait(group, block, part)
-                gsend[group, step, part] = (
-                    grown(step, part) + grecv[group, block, part].astype(F32)
+                grad_copy(group, step, part).start()
+
+        if relay and step == 0:
+            pl.when(outer)(go)
+        else:
+            go()
+
+    def pass_on(group):
+        def go():
+            for part in range(2):
+                grad_wait(group, nt, part)
+                gsend[group, 0, part] = (
+                    grown(0, part) + grecv[group, nt, part].astype(F32)
                 ).astype(BF16)
-                copy.start()
-
-            pl.when(relayed)(go)
+                grad_copy(group, 0, part).start()
+
+        if relay:
+            pl.when(inner)(go)
 
     def h_copy(step, group, part):
         mine = hall.at[hd, group, part]
@@ -392,13 +398,17 @@
     def own_grad(group):
         for part in range(2):
             gpart[nt - 1, part] = grown(nt - 1, part)
-            for there, place in ((txt > 0, txt), (txt < nt - 1, jnp.int32(nt))):
-
-                def add(place=place, part=part):
-                    grad_wait(group, place, part)
-                    gpart[nt - 1, part] = gpart[nt - 1, part] + grecv[group, place, part].astype(F32)
-
-                pl.when(there)(add)
+
+            def add(step, part=part):
+                place = block_at(step)
+                grad_wait(group, place, part)
+                gpart[nt - 1, part] = gpart[nt - 1, part] + grecv[group, place, part].astype(F32)
+
+            for step in range(1, nt):
+                if relay and step == nt - 1:
+                    pl.when(inner)(functools.partial(add, step))
+                else:
+                    add(step)
             hall[hd, group, part] = gpart[nt - 1, part].T.astype(BF16)
             for step in range(1, nh):
                 h_copy(step, group, part).start()
@@ -492,61 +502,61 @@
             for part in range(2):
                 h_copy(step, group, part).wait_recv()
 
-    for part in range(2):
-        own_sum(0, part)
-
-        def go(part=part, side=0):
-            kv_copy(0, part, side).start()
-
-        for side in range(2):
-            pl.when(has_side[side])(functools.partial(go, part, side))
     q_load.wait()
     g_load.wait()
     turn_over(0)
+    for part in range(2):
+        own_sum(0, part)
+        send_own(0, [part])
     forward(0, txt, True)
     for part in range(2):
         own_sum(1, part)
-    send_own(1, 0)
-    for step in range(1, nt):
+    if relay:
+        pl.when(outer)(lambda: send_own(1, range(2)))
+    for step in range(1, nt - 1):
         receive(0, step)
-        send_own(1, step)
-        forward(0, arrival(0, step)[0], False)
+        forward(0, block_at(step), False)
         if step == 1:
             turn_over(1)
+    pass_block(0, lambda: send_own(1, range(2)))
+    receive_last(0)
+    forward(0, block_at(nt - 1), False)
     stats_start(0)
     forward(1, txt, True)
     receive(1, 1)
+    forward(1, block_at(1), False)
     stats_finish(0)
-    for step in range(nt - 1):
+    backward(0, 0)
+    leave(0, 0)
+    backward(0, 1)
+    leave(0, 1)
+    pass_block(1)
+    pass_on(0)
+    for step in range(2, nt - 1):
+        receive(1, step)
+        forward(1, block_at(step), False)
         backward(0, step)
         leave(0, step)
-        if step + 2 < nt:
-            receive(1, step + 2)
-        if step >= 1:
-            pass_on(0, step - 1)
-    for step in range(1, nt):
-        forward(1, arrival(1, step)[0], False)
-    stats_start(1)
-    pass_on(0, nt - 2)
     backward(0, nt - 1)
     outputs(0)
+    receive_last(1)
+    forward(1, block_at(nt - 1), False)
+    stats_start(1)
+    own_grad(0)
+    cross(0)
     stats_finish(1)
     for step in range(nt - 1):
-        if step == 1:
-            own_grad(0)
-            outputs(1)
-            cross(0)
         backward(1, step)
         leave(1, step)
-        if step >= 1:
-            pass_on(1, step - 1)
+        if step == 1:
+            pass_on(1)
+    outputs(1)
     backward(1, nt - 1)
-    pass_on(1, nt - 2)
-    cross(1)
     share(0)
     h_wait(0)
     owners = [hd] + [other(step) for step in range(1, nh)]
     features([(o, 0) for o in owners], True, False)
+    cross(1)
     own_grad(1)
     features([(hd, 1)], False, False)
     share(1)
@@ -558,26 +568,15 @@
     for copy in p_copies.values():
         copy.wait_send()
     for group in range(groups):
-        for side in range(2):
-
-            def own_sent(group=group, side=side):
-                for part in range(2):
-                    kv_copy(group, part, side).wait_send()
-
-            pl.when(has_side[side])(own_sent)
-        for step in range(1, nt):
-            _, valid, copies = arrival(group, step)
-
-            def passed(copies=copies):
-                for copy in copies:
-                    copy.wait_send()
-
-            pl.when(valid)(passed)
+        for part in range(2):
+            for valid, copy in own_copies(group, part):
+                pl.when(valid)(copy.wait_send)
+            if relay:
+                pl.when(inner)(relay_copy(group, part).wait_send)
+            for step in range(nt - 1):
+                grad_copy(group, step, part).wait_send()
         for copy in stats_copies(group):
             copy.wait_send()
-        for step in range(nt - 1):
-            for part in range(2):
-                grad_copy(group, step, part)[0].wait_send()
         pair_copy(group).wait_send()
         for bit in range(1, bits):
             cross_copy(group, bit).wait_send()
@@ -646,7 +645,7 @@
             pltpu.VMEM((groups, crosses, half, gcols), BF16),
             dma((3,)), dma((nh, groups, 2)),
             dma((nh - 1, groups, 2)), dma((nh - 1, groups, 2)),
-            dma((groups, 2, 2)), dma((groups, nt, 2)), dma((groups, nt, 2)),
+            dma((groups, 2, nt - 1)), dma((groups, 2)), dma((groups, nt, 2)),
             dma((groups, ni - 1)), dma((groups, ni - 1)),
             dma((groups,)), dma((groups,)),
             dma((groups, crosses)), dma((groups, crosses)),

time: 69.3 us -> 73.2 us (1.056)
  Pallas kernels: 65.5 us -> 70.1 us
    pallas_call x1, Pallas kernels: 65.5 us -> 70.1 us  [shards(): pl.pallas_call(functools.partial(kernel, sizes, keep), out_shape=(pltpu.V...]
where the time goes in v2:
time: 73.2 us; the launch traced here: 73 us
  Pallas kernels  70.1 us (96%)
  local copies, waits for them, and re-layouts  2.24 us (3%)
    pallas_call x1, Pallas kernels, shards(): pl.pallas_call(functools.partial(kernel, sizes, keep), out_shape=(pltpu.V...  70.1 us
    unnamed x2, local copies, waits for them, and re-layouts  2.24 us

profile of v2, /device:TPU:0, one launch (start us, length us, event | category | flops | bytes accessed | tf_op | source)
XLA Modules:
  0.0 73.0 jit_solution(17614326003513928683)
XLA Ops:
  0.6 70.1 %shard_map.86 = (bf16[256,2048]{1,0:T(8,128)(2,1)S(1)}, bf16[256,3840]{1,0:T(8,128)(2,1)S(1)}) custom-call(bf16[256,3840]{1,0:T(8,128)(2,1)} %feats_hbm.1, bf16[3840,512]{1,0:T(8,128)(2,1)} %kw_hbm.1, bf16[3840,512]{1,0:T(8,128)(2,1)} %vw_hbm.1, bf16[256,2048]{1,0:T(8,128)(2,1)} %q_hbm.1, bf16[256,2048]{1,0:T(8,128)(2,1)} %g_hbm.1, s32[8]{0:T(128)} %tile_image.1, ...), custom_call_target="tpu_custom_call" | custom-call | tf_op jit(solution)/shard_map/pallas_call | solution.py:609
  70.7 1.0 %copy.11 = bf16[256,2048]{1,0:T(8,128)(2,1)} copy(bf16[256,2048]{1,0:T(8,128)(2,1)S(1)} %get-tuple-element.2) | data formatting | bytes 2097152
  71.7 1.3 %copy.12 = bf16[256,3840]{1,0:T(8,128)(2,1)} copy(bf16[256,3840]{1,0:T(8,128)(2,1)S(1)} %get-tuple-element.3) | data formatting | bytes 3932160

commit v3 on v1

--- a/solution.py
+++ b/solution.py
@@ -12,7 +12,7 @@
 TILE = 128
 TBLK = 128
 MESH = pl.DeviceIdType.MESH
-UNROLL = 4
+UNROLL = 8
 LOG2E = 1.4426950408889634
 NT = (((1,), (1,)), ((), ()))
 F32 = jnp.float32
@@ -47,9 +47,9 @@
 
 def kernel(
     sizes, keep,
-    feats_hbm, kw_hbm, vw_hbm, q_hbm, g_hbm, tile_image, text_sees,
+    feats_hbm, kw_hbm, vw_hbm, q_hbm, g_hbm, tiles_hbm, sees_hbm,
     attn, dfeats,
-    feats, kw, vw, qraw, graw, qt, gt, big, psend, precv, pacc, kvbuf, vtb, sbuf, numt, mst, tst,
+    tile_image, text_sees, feats, kw, vw, qraw, graw, qt, gt, big, psend, precv, pacc, kvbuf, vtb, sbuf, numt, mst, tst,
     stbuf, lse, dlt, cown, gsend, grecv, gpart, hall, ocr, xs, xr,
     l_s, w_s, p_ss, p_rs, kv_ss, kv_fs, kv_rs, st_ss, st_rs, oc_ss, oc_rs, ox_ss, ox_rs,
     oa_ss, oa_rs, g_ss, g_rs, h_ss, h_rs,
@@ -89,7 +89,11 @@
             loads += pair
     q_load = pltpu.make_async_copy(q_hbm, qraw, l_s.at[1])
     g_load = pltpu.make_async_copy(g_hbm, graw, l_s.at[2])
-    loads += [q_load, g_load]
+    tables = [
+        pltpu.make_async_copy(tiles_hbm, tile_image, l_s.at[3]),
+        pltpu.make_async_copy(sees_hbm, text_sees, l_s.at[4]),
+    ]
+    loads += [q_load, g_load] + tables
     for copy in loads:
         copy.start()
 
@@ -107,15 +111,6 @@
             device_id={axis: index}, device_id_type=MESH,
         )
 
-    first_block = txt * (text // TBLK)
-    for tile in range(big.shape[0]):
-        image = tile_image[tile]
-        parts = [
-            jnp.full((1, TBLK), text_sees[first_block + at, image].astype(F32))
-            for at in range(text // TBLK)
-        ]
-        seen = jnp.concatenate(parts, axis=1)
-        big[pl.ds(tile, 1), :] = jnp.where(seen > 0.5, 0.0, HIDE)
     vtb[pl.ds(HD, ONES), :] = jnp.ones((ONES, rows), BF16)
 
     def project(step, group):
@@ -143,6 +138,18 @@
     for group in range(groups):
         pacc[group] = project(0, group)
 
+    for copy in tables:
+        copy.wait()
+    first_block = txt * (text // TBLK)
+    for tile in range(big.shape[0]):
+        image = tile_image[tile]
+        parts = [
+            jnp.full((1, TBLK), text_sees[first_block + at, image].astype(F32))
+            for at in range(text // TBLK)
+        ]
+        seen = jnp.concatenate(parts, axis=1)
+        big[pl.ds(tile, 1), :] = jnp.where(seen > 0.5, 0.0, HIDE)
+
     def kv_copy(group, part, side):
         mine = kvbuf.at[group, txt, part]
         return remote(
@@ -196,6 +203,25 @@
         for copy in copies:
             copy.wait_recv()
             pl.when(valid)(copy.start)
+
+    def pass_block(group, step):
+        _, valid, copies = arrival(group, step)
+
+        def go():
+            for copy in copies:
+                copy.wait_recv()
+                copy.start()
+
+        pl.when(valid)(go)
+
+    def take(group, step):
+        _, valid, copies = arrival(group, step)
+
+        def go():
+            for copy in copies:
+                copy.wait_recv()
+
+        pl.when(jnp.logical_not(valid))(go)
 
     def turn_over(group):
         def body(at, _):
@@ -277,7 +303,8 @@
             )
             return 0
 
-        lax.fori_loop(0, reps, deltas, 0)
+        for at in range(reps):
+            deltas(at, 0)
         stbuf[group, img, 0] = mst[group_rows(group), :]
         stbuf[group, img, 1] = tst[group_rows(group), :]
         for copy in stats_copies(group):
@@ -346,19 +373,19 @@
             picked = [group * reps + a for a in at]
             queries = jnp.concatenate([qt[head] for head in picked], axis=1)
             grads = jnp.concatenate([gt[head] for head in picked], axis=1)
-            gpart[step, 0] = gpart[step, 0] + lax.dot_general(
+            gpart[group, step, 0] = gpart[group, step, 0] + lax.dot_general(
                 queries, jnp.concatenate(grads_all, axis=1), NT, preferred_element_type=F32
             )
-            gpart[step, 1] = gpart[step, 1] + lax.dot_general(
+            gpart[group, step, 1] = gpart[group, step, 1] + lax.dot_general(
                 grads, jnp.concatenate(probs_all, axis=1), NT, preferred_element_type=F32
             )
             return 0
 
-        gpart[step] = jnp.zeros_like(gpart[step])
+        gpart[group, step] = jnp.zeros((2, HD, rows), F32)
         lax.fori_loop(0, reps // unroll, body, 0)
 
-    def grown(step, part):
-        value = gpart[step, part]
+    def grown(group, step, part):
+        value = gpart[group, step, part]
         return value * scale if part == 0 else value
 
     def leave(group, step):
@@ -366,7 +393,7 @@
             copy, relayed, _ = grad_copy(group, step, part)
 
             def go(copy=copy, part=part):
-                gsend[group, step, part] = grown(step, part).astype(BF16)
+                gsend[group, step, part] = grown(group, step, part).astype(BF16)
                 copy.start()
 
             pl.when(jnp.logical_not(relayed))(go)
@@ -378,7 +405,7 @@
             def go(copy=copy, part=part, block=block):
                 grad_wait(group, block, part)
                 gsend[group, step, part] = (
-                    grown(step, part) + grecv[group, block, part].astype(F32)
+                    grown(group, step, part) + grecv[group, block, part].astype(F32)
                 ).astype(BF16)
                 copy.start()
 
@@ -391,15 +418,15 @@
 
     def own_grad(group):
         for part in range(2):
-            gpart[nt - 1, part] = grown(nt - 1, part)
+            gpart[group, nt - 1, part] = grown(group, nt - 1, part)
             for there, place in ((txt > 0, txt), (txt < nt - 1, jnp.int32(nt))):
 
                 def add(place=place, part=part):
                     grad_wait(group, place, part)
-                    gpart[nt - 1, part] = gpart[nt - 1, part] + grecv[group, place, part].astype(F32)
+                    gpart[group, nt - 1, part] = gpart[group, nt - 1, part] + grecv[group, place, part].astype(F32)
 
                 pl.when(there)(add)
-            hall[hd, group, part] = gpart[nt - 1, part].T.astype(BF16)
+            hall[hd, group, part] = gpart[group, nt - 1, part].T.astype(BF16)
             for step in range(1, nh):
                 h_copy(step, group, part).start()
 
@@ -435,7 +462,8 @@
             qraw[:, cols] = (numt[head] * cown[pl.ds(head, 1), :]).T.astype(BF16)
             return 0
 
-        lax.fori_loop(0, reps, body, 0)
+        for at in range(reps):
+            body(at, 0)
         pair_copy(group).start()
 
     def cross(group):
@@ -507,49 +535,65 @@
     for part in range(2):
         own_sum(1, part)
     send_own(1, 0)
-    for step in range(1, nt):
-        receive(0, step)
-        send_own(1, step)
-        forward(0, arrival(0, step)[0], False)
-        if step == 1:
-            turn_over(1)
+    pass_block(0, 1)
+    send_own(1, 1)
+    pass_block(0, 2)
+    send_own(1, 2)
+    take(0, 1)
+    forward(0, arrival(0, 1)[0], False)
+    turn_over(1)
+    pass_block(0, 3)
+    send_own(1, 3)
+    take(0, 2)
+    forward(0, arrival(0, 2)[0], False)
+    take(0, 3)
+    forward(0, arrival(0, 3)[0], False)
     stats_start(0)
     forward(1, txt, True)
-    receive(1, 1)
+    pass_block(1, 1)
     stats_finish(0)
-    for step in range(nt - 1):
-        backward(0, step)
-        leave(0, step)
-        if step + 2 < nt:
-            receive(1, step + 2)
-        if step >= 1:
-            pass_on(0, step - 1)
-    for step in range(1, nt):
-        forward(1, arrival(1, step)[0], False)
+    backward(0, 0)
+    leave(0, 0)
+    pass_block(1, 2)
+    take(1, 1)
+    forward(1, arrival(1, 1)[0], False)
+    backward(0, 1)
+    leave(0, 1)
+    pass_block(1, 3)
+    pass_on(0, 0)
+    take(1, 2)
+    forward(1, arrival(1, 2)[0], False)
+    take(1, 3)
+    forward(1, arrival(1, 3)[0], False)
     stats_start(1)
-    pass_on(0, nt - 2)
-    backward(0, nt - 1)
+    backward(0, 2)
+    leave(0, 2)
+    pass_on(0, 1)
     outputs(0)
     stats_finish(1)
-    for step in range(nt - 1):
-        if step == 1:
-            own_grad(0)
-            outputs(1)
-            cross(0)
-        backward(1, step)
-        leave(1, step)
-        if step >= 1:
-            pass_on(1, step - 1)
-    backward(1, nt - 1)
-    pass_on(1, nt - 2)
+    backward(1, 0)
+    leave(1, 0)
+    cross(0)
+    pass_on(0, 2)
+    backward(1, 1)
+    leave(1, 1)
+    backward(0, 3)
+    backward(1, 2)
+    leave(1, 2)
+    outputs(1)
+    pass_on(1, 0)
     cross(1)
+    backward(1, 3)
+    own_grad(0)
+    pass_on(1, 1)
+    pass_on(1, 2)
     share(0)
     h_wait(0)
     owners = [hd] + [other(step) for step in range(1, nh)]
     features([(o, 0) for o in owners], True, False)
+    share(1)
     own_grad(1)
     features([(hd, 1)], False, False)
-    share(1)
     finish_output(0)
     finish_output(1)
     h_wait(1)
@@ -585,6 +629,17 @@
         for step in range(1, nh):
             for part in range(2):
                 h_copy(step, group, part).wait_send()
+
+
+def flush(attn_ready, feats_ready, attn, feats, sems):
+    copies = [
+        pltpu.make_async_copy(attn_ready, attn, sems.at[0]),
+        pltpu.make_async_copy(feats_ready, feats, sems.at[1]),
+    ]
+    for copy in copies:
+        copy.start()
+    for copy in copies:
+        copy.wait()
 
 
 def shards(sizes, image_feats, key_weight, value_weight, queries, grad_out, tile_image, text_sees):
@@ -606,16 +661,17 @@
     dma = pltpu.SemaphoreType.DMA
     hbm = pl.BlockSpec(memory_space=pl.ANY)
     vmem = pl.BlockSpec(memory_space=pltpu.VMEM)
-    smem = pl.BlockSpec(memory_space=pltpu.SMEM)
     attn, grad_feats = pl.pallas_call(
         functools.partial(kernel, sizes, keep),
         out_shape=(
             pltpu.VMEM((text, width), BF16),
             pltpu.VMEM(image_feats.shape, BF16),
         ),
-        in_specs=[hbm] * 5 + [smem] * 2,
+        in_specs=[hbm] * 7,
         out_specs=(vmem, vmem),
         scratch_shapes=[
+            pltpu.SMEM(tile_image.shape, tile_image.dtype),
+            pltpu.SMEM(text_sees.shape, text_sees.dtype),
             pltpu.VMEM(image_feats.shape, BF16),
             pltpu.VMEM(key_weight.shape, BF16),
             pltpu.VMEM(value_weight.shape, BF16),
@@ -639,12 +695,12 @@
             pltpu.VMEM((heads, text), F32),
             pltpu.VMEM((groups, nt - 1, 2, HD, rows), BF16),
             pltpu.VMEM((groups, nt + 1, 2, HD, rows), BF16),
-            pltpu.VMEM((nt, 2, HD, rows), F32),
+            pltpu.VMEM((groups, nt, 2, HD, rows), F32),
             pltpu.VMEM((nh, groups, 2, rows, HD), BF16),
             pltpu.VMEM((groups, half, gcols), BF16),
             pltpu.VMEM((groups, crosses, half, gcols), BF16),
             pltpu.VMEM((groups, crosses, half, gcols), BF16),
-            dma((3,)), dma((nh, groups, 2)),
+            dma((5,)), dma((nh, groups, 2)),
             dma((nh - 1, groups, 2)), dma((nh - 1, groups, 2)),
             dma((groups, 2, 2)), dma((groups, nt, 2)), dma((groups, nt, 2)),
             dma((groups, ni - 1)), dma((groups, ni - 1)),
@@ -658,7 +714,19 @@
             collective_id=0, has_side_effects=True, vmem_limit_bytes=VMEM_BUDGET
         ),
     )(image_feats, key_weight, value_weight, queries, grad_out, tile_image, text_sees)
-    return (attn, grad_feats)
+    return pl.pallas_call(
+        flush,
+        out_shape=(
+            jax.ShapeDtypeStruct((text, width), BF16),
+            jax.ShapeDtypeStruct(image_feats.shape, BF16),
+        ),
+        in_specs=[hbm] * 2,
+        out_specs=(hbm, hbm),
+        scratch_shapes=[dma((2,))],
+    )(
+        pltpu.with_memory_space_constraint(attn, pltpu.VMEM),
+        pltpu.with_memory_space_constraint(grad_feats, pltpu.VMEM),
+    )
 
 
 def solution(mesh):

time: 69.3 us -> 61.4 us (0.89); the launches traced: 68.4 us -> 61.3 us
  Pallas kernels: 65.5 us -> 60.5 us
  local copies, waits for them, and re-layouts: 2.24 us -> 0 us
    pallas_call x1, Pallas kernels: 65.5 us -> 58.8 us  [shards(): pl.pallas_call(functools.partial(kernel, sizes, keep), out_shape=(pltpu.V...]
    unnamed x2 -> x0, local copies, waits for them, and re-layouts: 2.24 us -> none
    pallas_call x0 -> x1, Pallas kernels: none -> 1.64 us  [shards(): pl.pallas_call(flush, out_shape=(jax.ShapeDtypeStruct((text, width), BF16...]
where the time goes in v3:
time: 61.4 us; the launch traced here: 61.3 us
  Pallas kernels  60.5 us (99%)
  between operations  0.8 us (1%)
    pallas_call x1, Pallas kernels, shards(): pl.pallas_call(functools.partial(kernel, sizes, keep), out_shape=(pltpu.V...  58.8 us
    pallas_call x1, Pallas kernels, shards(): pl.pallas_call(flush, out_shape=(jax.ShapeDtypeStruct((text, width), BF16...  1.64 us

profile of v3, /device:TPU:0, one launch (start us, length us, event | category | flops | bytes accessed | tf_op | source)
XLA Modules:
  0.0 61.3 jit_solution(9293559473915365513)
XLA Ops:
  0.6 58.8 %shard_map.86 = (bf16[256,2048]{1,0:T(8,128)(2,1)S(1)}, bf16[256,3840]{1,0:T(8,128)(2,1)S(1)}) custom-call(bf16[256,3840]{1,0:T(8,128)(2,1)} %feats_hbm.1, bf16[3840,512]{1,0:T(8,128)(2,1)} %kw_hbm.1, bf16[3840,512]{1,0:T(8,128)(2,1)} %vw_hbm.1, bf16[256,2048]{1,0:T(8,128)(2,1)} %q_hbm.1, bf16[256,2048]{1,0:T(8,128)(2,1)} %g_hbm.1, s32[8]{0:T(128)} %tiles_hbm.1, ...), custom_call_target="tpu_custom_call" | custom-call | tf_op jit(solution)/shard_map/pallas_call | solution.py:664
  59.5 1.6 %shard_map.87 = (bf16[256,2048]{1,0:T(8,128)(2,1)}, bf16[256,3840]{1,0:T(8,128)(2,1)}) custom-call(bf16[256,2048]{1,0:T(8,128)(2,1)S(1)} %get-tuple-element.4.attn_ready, bf16[256,3840]{1,0:T(8,128)(2,1)S(1)} %get-tuple-element.5.feats_ready), custom_call_target="tpu_custom_call" | custom-call | tf_op jit(solution)/shard_map/pallas_call | solution.py:717
